TPU v7x, 32 devices: a whole 2x2x4 slice. The times are simulated.
32 devices in a mesh: seq: 4 (over y, x), exp: 8 (over z, core).
Axes of the slice: x: 2, y: 2, z: 4, core: 2. Of those that a mesh axis runs over, the one named last changes fastest.
Arguments:
- tokens: bfloat16 [2, 24576, 1024], P(None, ('seq', 'exp')), may hold values from -60 to 60
- router: bfloat16 [1024, 64], replicated, may hold values from -0.25 to 0.25
- w_in: bfloat16 [16, 1024, 4096], P('exp', None, 'seq'), may hold values from -0.1875 to 0.1875
- w_out: bfloat16 [16, 4096, 1024], P('exp', 'seq'), may hold values from -0.09375 to 0.09375
- grad_out: bfloat16 [2, 24576, 1024], P(None, ('seq', 'exp')), may hold values from -6 to 6
Outputs:
- mixed: bfloat16 [2, 24576, 1024], P(None, ('seq', 'exp'))
- grad_tokens: bfloat16 [2, 24576, 1024], P(None, ('seq', 'exp'))
- grad_router: float32 [1024, 64], P(('seq', 'exp'))
- grad_w_in: bfloat16 [16, 1024, 4096], P('exp', None, 'seq')
- grad_w_out: bfloat16 [16, 4096, 1024], P('exp', 'seq')
All inputs are finite; a program needn't handle non-finite values.
Results may differ from a plain program's by a relative error of at most 0.018.
Values may be sent and summed in bfloat16 or wider, within the bound.
A program may use at most 128 MiB of HBM per device.

v0:
```python
import jax
import jax.numpy as jnp
from jax import lax
from jax.sharding import PartitionSpec as P


def on_device(tokens, router, w_in, w_out, grad_out):
    clips, tok_rows, width = tokens.shape
    slot_total = router.shape[1]
    owned = slot_total // lax.axis_size("exp")
    experts_here = w_in.shape[0]
    per_expert = owned // experts_here
    logits = jnp.dot(
        tokens.reshape(clips * tok_rows, width), router, preferred_element_type=jnp.float32
    ).reshape(clips, tok_rows, slot_total)
    slot_peak = lax.pmax(jnp.max(logits, axis=1), ("seq", "exp"))
    exp_terms = jnp.exp(logits - slot_peak[:, None, :])
    slot_mass = lax.psum(jnp.sum(exp_terms, axis=1), ("seq", "exp"))
    dispatch = exp_terms / slot_mass[:, None, :]
    dispatch_b = dispatch.astype(jnp.bfloat16)
    mixing = jax.nn.softmax(logits, axis=2)
    mixing_b = mixing.astype(jnp.bfloat16)
    inputs = jnp.einsum("cts,ctd->scd", dispatch_b, tokens, preferred_element_type=jnp.float32)
    grads = jnp.einsum("cts,ctd->scd", mixing_b, grad_out, preferred_element_type=jnp.float32)
    summed = lax.psum(jnp.concatenate([inputs, grads], axis=1), ("seq", "exp"))
    owner_sums = lax.dynamic_slice_in_dim(summed, lax.axis_index("exp") * owned, owned, 0)
    expert_rows = (
        owner_sums[:, :clips].astype(jnp.bfloat16).reshape(experts_here, per_expert * clips, width)
    )
    grad_rows = (
        owner_sums[:, clips:].astype(jnp.bfloat16).reshape(experts_here, per_expert * clips, width)
    )
    pre = jnp.einsum("erd,edh->erh", expert_rows, w_in, preferred_element_type=jnp.float32)
    hidden = jax.nn.gelu(pre).astype(jnp.bfloat16)
    expert_part = jnp.einsum("erh,ehd->erd", hidden, w_out, preferred_element_type=jnp.float32)
    hidden_grad = jnp.einsum("erd,ehd->erh", grad_rows, w_out, preferred_element_type=jnp.float32)
    pre_grad = jax.vjp(jax.nn.gelu, pre)[1](hidden_grad)[0].astype(jnp.bfloat16)
    grad_w_out = jnp.einsum(
        "erh,erd->ehd", hidden, grad_rows, preferred_element_type=jnp.float32
    ).astype(jnp.bfloat16)
    grad_w_in = jnp.einsum(
        "erd,erh->edh", expert_rows, pre_grad, preferred_element_type=jnp.float32
    ).astype(jnp.bfloat16)
    input_part = jnp.einsum("erh,edh->erd", pre_grad, w_in, preferred_element_type=jnp.float32)
    out_sums, in_sums = (
        lax.psum(expert_part.astype(jnp.bfloat16), "seq").astype(jnp.float32),
        lax.psum(input_part.astype(jnp.bfloat16), "seq").astype(jnp.float32),
    )
    slot_outputs = out_sums.astype(jnp.bfloat16).reshape(owned, clips, width)
    slot_in_grads = in_sums.astype(jnp.bfloat16).reshape(owned, clips, width)
    shard_rows = lax.all_gather(slot_outputs, "exp", axis=0, tiled=True)
    weights = mixing_b
    outputs = jnp.einsum("cts,scd->ctd", weights, shard_rows, preferred_element_type=jnp.float32)
    block = jnp.einsum("ctd,scd->cts", grad_out, shard_rows, preferred_element_type=jnp.float32)
    mixed = outputs
    mixing_grad = block
    shard_rows = lax.all_gather(slot_in_grads, "exp", axis=0, tiled=True)
    weights = dispatch_b
    outputs = jnp.einsum("cts,scd->ctd", weights, shard_rows, preferred_element_type=jnp.float32)
    block = jnp.einsum("ctd,scd->cts", tokens, shard_rows, preferred_element_type=jnp.float32)
    inner = lax.psum(jnp.sum(dispatch * block, axis=1), ("seq", "exp"))
    logit_grad = dispatch * (block - inner[:, None, :]) + mixing * (
        mixing_grad - jnp.sum(mixing * mixing_grad, axis=2, keepdims=True)
    )
    logit_b = logit_grad.astype(jnp.bfloat16)
    router_part = jnp.dot(
        logit_b.reshape(clips * tok_rows, slot_total), router.T, preferred_element_type=jnp.float32
    ).reshape(clips, tok_rows, width)
    grad_tokens = (outputs + router_part).astype(jnp.bfloat16)
    grad_router = lax.psum_scatter(
        jnp.einsum("ctd,cts->ds", tokens, logit_b, preferred_element_type=jnp.float32),
        ("seq", "exp"),
        scatter_dimension=0,
        tiled=True,
    )
    return (mixed.astype(jnp.bfloat16), grad_tokens, grad_router, grad_w_in, grad_w_out)


def solution(mesh):
    return jax.shard_map(
        on_device,
        mesh=mesh,
        in_specs=(
            P(None, ("seq", "exp"), None),
            P(),
            P("exp", None, "seq"),
            P("exp", "seq", None),
            P(None, ("seq", "exp"), None),
        ),
        out_specs=(
            P(None, ("seq", "exp"), None),
            P(None, ("seq", "exp"), None),
            P(("seq", "exp"), None),
            P("exp", None, "seq"),
            P("exp", "seq", None),
        ),
        check_vma=False,
    )
```

profile of v0, /device:TPU:0, one launch (start us, length us, event | category | flops | bytes accessed | tf_op | source)
XLA Modules:
  0.0 442.6 jit_solution(9276342582157628203)
XLA Ops:
  7.2 1.8 copy-done
  9.1 2.1 fusion.37
  12.0 41.9 %pmax.7 = f32[2,64]{1,0:T(2,128)S(1)} all-reduce(f32[2,64]{1,0:T(2,128)S(1)} %get-tuple-element.26), channel_id=1, replica_groups=mesh['seq'=4,'exp'=8] {'seq','exp'}, use_global_device_ids=true, to_apply=%region_3.0 | all-reduce | flops 128 | bytes 1024 | tf_op jit(solution)/shard_map/pmax | solution.py:16
  54.7 40.3 %psum.35 = f32[2,64]{1,0:T(2,128)S(1)} all-reduce(f32[2,64]{1,0:T(2,128)} %fusion.13), channel_id=1, replica_groups=mesh['seq'=4,'exp'=8] {'seq','exp'}, use_global_device_ids=true, to_apply=%region_5.0 | all-reduce | flops 128 | bytes 1024 | tf_op jit(solution)/shard_map/psum | solution.py:18
  95.0 1.5 convolution_bitcast_fusion.1
  96.5 3.4 convolution_bitcast_fusion
  99.9 2.4 pad_maximum_fusion
  102.3 49.9 %all-reduce.5 = bf16[64,4,1024]{2,0,1:T(8,128)(2,1)} all-reduce(f32[64,4,1024]{2,0,1:T(8,128)} %pad_maximum_fusion), channel_id=1, replica_groups=mesh['seq'=4,'exp'=8] {'seq','exp'}, use_global_device_ids=true, to_apply=%region_6.0 | all-reduce | flops 262144 | bytes 1572864 | tf_op jit(solution)/shard_map/psum | solution.py:25
  154.3 1.4 reshape.38
  155.7 1.4 copy.18
  157.1 1.4 reshape.36
  158.4 3.5 fusion.38
  162.0 3.5 fusion.28
  167.4 1.4 reshape.37
  168.8 1.4 copy.19
  170.1 4.0 convolution_convert_fusion.3
  174.2 1.4 reshape.39
  175.5 1.4 copy.21
  177.0 4.2 convolution_convert_fusion
  181.2 3.3 convolution_convert_fusion.1
  184.5 33.1 %all-reduce.4.cloned.1.call-done = (bf16[8,2,1024]{2,0,1:T(8,128)(2,1)}, bf16[8,2,1024]{2,0,1:T(8,128)(2,1)}) async-done(((bf16[8,2,1024]{2,0,1:T(8,128)(2,1)}, bf16[8,2,1024]{2,0,1:T(8,128)(2,1)}), (bf16[8,2,1024]{2,0,1:T(8,128)(2,1)}, bf16[8,2,1024]{2,0,1:T(8,128)(2,1)})) %all-reduce.4.cloned.1.call-update) | async-done | bytes 65552 | tf_op jit(solution)/shard_map/psum | solution.py:46
  217.6 14.6 %all_gather.7 = bf16[64,2,1024]{2,0,1:T(8,128)(2,1)S(1)} all-gather(bf16[8,2,1024]{2,0,1:T(8,128)(2,1)} %get-tuple-element.21), channel_id=1, replica_groups=mesh['seq'=4,'exp'=8] {'exp'}, dimensions={0}, use_global_device_ids=true | all-gather | bytes 294912 | tf_op jit(solution)/shard_map/all_gather | solution.py:57
  232.2 3.8 fusion.17
  236.0 2.4 multiply_reduce_fusion.1
  238.4 14.2 %all_gather.6 = bf16[64,2,1024]{2,0,1:T(8,128)(2,1)S(1)} all-gather(bf16[8,2,1024]{2,0,1:T(8,128)(2,1)S(1)} %copy-done.8), channel_id=1, replica_groups=mesh['seq'=4,'exp'=8] {'exp'}, dimensions={0}, use_global_device_ids=true | all-gather | bytes 294912 | tf_op jit(solution)/shard_map/all_gather | solution.py:51
  252.6 1.8 convolution_bitcast_fusion.2
  254.4 39.4 %psum.39 = f32[2,64]{1,0:T(2,128)} all-reduce(f32[2,64]{1,0:T(2,128)} %get-tuple-element.30), channel_id=1, replica_groups=mesh['seq'=4,'exp'=8] {'seq','exp'}, use_global_device_ids=true, to_apply=%region_10.0 | all-reduce | flops 128 | bytes 1024 | tf_op jit(solution)/shard_map/psum | solution.py:61
  293.8 3.0 convolution_bitcast_fusion.4
  296.8 2.0 copy.23
  298.8 3.7 convolution_convert_fusion.2
  302.5 6.2 %add_convert_fusion = bf16[2,768,1024]{2,1,0:T(8,128)(2,1)} fusion(f32[2,768,1024]{2,1,0:T(8,128)} %fusion.17, f32[2,768,64]{1,2,0:T(8,128)} %convolution_bitcast_fusion.2, f32[2,768,64]{1,2,0:T(8,128)} %get-tuple-element.31, f32[2,64]{1,0:T(2,128)} %psum.39, bf16[1024,64]{0,1:T(8,128)(2,1)} %param.6, f32[2,768,64]{1,2,0:T(8,128)} %get-tuple-element.25, ...), kind=kOutput, calls=%fused_computation.2 | convolution fusion | flops 205555264 | bytes 11148800 | tf_op jit(solution)/shard_map/dot_general | solution.py:66
  308.7 127.1 %reduce-scatter.4.cloned.1.call-done = f32[32,64]{1,0:T(8,128)} async-done(((f32[1024,64]{1,0:T(8,128)}), f32[32,64]{1,0:T(8,128)}) %reduce-scatter.4.cloned.1.call-update) | async-done | bytes 8208
  (27 shorter events, 5.8 us)
Async XLA Ops:
  7.2 1.9 copy-start
  7.2 210.4 %all-reduce.4.cloned.1.call-start = ((), (), s32[]{:S(2)}) async-start(), calls=%async_computation.2 | async-start | bytes 131072 | tf_op jit(solution)/shard_map/psum | solution.py:46
  158.4 3.5 copy-start.6
  158.4 7.7 %copy-start.1 = (bf16[2,1024,1024]{2,1,0:T(8,128)(2,1)S(1)}, bf16[2,1024,1024]{2,1,0:T(8,128)(2,1)}, u32[]{:S(2)}) copy-start(bf16[2,1024,1024]{2,1,0:T(8,128)(2,1)} %param.8) | copy-start | bytes 12582916
  165.5 0.6 copy-start.4
  176.9 258.9 %reduce-scatter.4.cloned.1.call-start = ((), (), s32[]{:S(2)}) async-start(), calls=%async_computation.1 | async-start | bytes 540672
  177.0 4.2 copy-start.5
  177.0 4.2 copy-start.7
  232.2 6.2 %copy-start.8 = (bf16[8,2,1024]{2,0,1:T(8,128)(2,1)S(1)}, bf16[8,2,1024]{2,0,1:T(8,128)(2,1)}, u32[]{:S(2)}) copy-start(bf16[8,2,1024]{2,0,1:T(8,128)(2,1)} %get-tuple-element.20) | copy-start | bytes 98308
  232.2 20.4 %copy-start.2 = (bf16[2,768,1024]{2,1,0:T(8,128)(2,1)S(1)}, bf16[2,768,1024]{2,1,0:T(8,128)(2,1)}, u32[]{:S(2)}) copy-start(bf16[2,768,1024]{2,1,0:T(8,128)(2,1)} %param.9) | copy-start | bytes 9437188
  252.6 1.8 copy-start.3
Sparse Core Ops, SparseCore 0:
  177.0 40.5 all-reduce.3
  298.9 136.8 reduce-scatter.3
where the time goes:
time: 444 us; the launch traced here: 443 us
  blocking collectives  200 us (45%)
  waiting for transfers between devices  160 us (36%)
  matrix products  47.6 us (11%)
  local copies, waits for them, and re-layouts  16.2 us (4%)
  between operations  14.1 us (3%)
    unnamed x3, waiting for transfers between devices  127 us
    psum x1, blocking collectives, on_device(): summed = lax.psum(jnp.concatenate([inputs, grads], axis=1), ('seq', 'exp'))  49.9 us
    pmax x1, blocking collectives, on_device(): slot_peak = lax.pmax(jnp.max(logits, axis=1), ('seq', 'exp'))  41.9 us
    psum x1, blocking collectives, on_device(): slot_mass = lax.psum(jnp.sum(exp_terms, axis=1), ('seq', 'exp'))  40.3 us
    psum x1, blocking collectives, on_device(): inner = lax.psum(jnp.sum(dispatch * block, axis=1), ('seq', 'exp'))  39.4 us
    psum x1, waiting for transfers between devices, on_device(): lax.psum(expert_part.astype(jnp.bfloat16), 'seq').astype(jnp.float32)  33.1 us
    all_gather x1, blocking collectives, on_device(): shard_rows = lax.all_gather(slot_in_grads, 'exp', axis=0, tiled=True)  14.6 us
    all_gather x1, blocking collectives, on_device(): shard_rows = lax.all_gather(slot_outputs, 'exp', axis=0, tiled=True)  14.2 us
  transfers between devices with their start and end apart: 2, of which 2 were waited for; matrix products, arithmetic and copies ran while one was open for 4% of the time, Pallas kernels for 0%

commit v1 on v0

v1 whole, which is shorter than its diff:
```python
import functools

import jax
import jax.numpy as jnp
from jax import lax
from jax.experimental import pallas as pl
from jax.experimental.pallas import tpu as pltpu
from jax.sharding import PartitionSpec as P

MESH = pl.DeviceIdType.MESH
F32 = jnp.float32
BF16 = jnp.bfloat16
NT = (((1,), (1,)), ((), ()))


def dot(a, b):
    return jnp.dot(a, b, preferred_element_type=F32)


def dot_nt(a, b):
    return lax.dot_general(a, b, NT, preferred_element_type=F32)


def place(seq_n, exp_n):
    s = lax.axis_index("seq")
    e = lax.axis_index("exp")
    h, par = e // 2, e % 2
    pair = (s, h * 2 + (1 - par))
    seq_peers = [((s + k) % seq_n, e) for k in range(1, seq_n)]
    exp_peers = [(s, ((h + k) % (exp_n // 2)) * 2 + par) for k in range(1, exp_n // 2)]
    return s, h, par, pair, seq_peers, exp_peers


def greet(peers):
    barrier = pltpu.get_barrier_semaphore()
    for peer in peers:
        pl.semaphore_signal(barrier, inc=1, device_id=peer, device_id_type=MESH)
    pl.semaphore_wait(barrier, len(peers))


class Sender:
    def __init__(self, send_sem, recv_sem):
        self.send_sem, self.recv_sem, self.count, self.open = send_sem, recv_sem, 0, []

    def start(self, src, dst, peer):
        copy = pltpu.make_async_remote_copy(
            src_ref=src,
            dst_ref=dst,
            send_sem=self.send_sem.at[self.count],
            recv_sem=self.recv_sem.at[self.count],
            device_id=peer,
            device_id_type=MESH,
        )
        copy.start()
        self.count += 1
        self.open.append(copy)
        return copy

    def drain(self):
        for copy in self.open:
            copy.wait_send()


def front_copies(seq_n, exp_n):
    half = exp_n // 2
    seq, rest = seq_n - 1, half - 1
    stats = 1 + seq + rest
    reduce = 1 + seq + rest + seq
    gather = seq + 2 * (rest + seq + 1)
    return stats + reduce + gather


def as_column(row, n):
    eye = lax.broadcasted_iota(jnp.int32, (n, n), 0) == lax.broadcasted_iota(jnp.int32, (n, n), 1)
    return jnp.sum(jnp.where(eye, jnp.broadcast_to(row, (n, n)), 0.0), axis=1, keepdims=True)


def as_row(column, n):
    eye = lax.broadcasted_iota(jnp.int32, (n, n), 0) == lax.broadcasted_iota(jnp.int32, (n, n), 1)
    return jnp.sum(jnp.where(eye, jnp.broadcast_to(column, (n, n)), 0.0), axis=0, keepdims=True)


def row_softmax(lg):
    q = jnp.exp(lg - jnp.max(lg, axis=1, keepdims=True))
    return q / jnp.sum(q, axis=1, keepdims=True)


def front(
    seq_n, exp_n, tok, rt, gout, win_hbm, wout_hbm,
    so_o, sg_o, st_o, x_o, g_o, hid_o, pg_o,
    win, wout, xt, qt, st_a, st_p, st_b, st_s, st_c, st_z,
    buf_a, rcv_a, buf_b, rcv_b, buf_c, rcv_c, xf, xg, buf_e, rcv_e, ag, inn, acc_p,
    w_sem, send_sem, recv_sem,
):
    clips, rows, width = tok.shape
    slots = rt.shape[1]
    half = exp_n // 2
    owned = slots // exp_n
    dc = width // seq_n
    kinds = 2 * clips
    experts = win.shape[0]
    s, h, par, pair, seq_peers, exp_peers = place(seq_n, exp_n)

    load_in = pltpu.make_async_copy(win_hbm, win, w_sem.at[0])
    load_out = pltpu.make_async_copy(wout_hbm, wout, w_sem.at[1])
    load_in.start()
    load_out.start()
    net = Sender(send_sem, recv_sem)

    peaks, masses = [], []
    for c in range(clips):
        lg = dot(tok[c], rt[...])
        m = jnp.max(lg, axis=0, keepdims=True)
        p = jnp.exp(lg - m)
        peaks.append(m)
        masses.append(jnp.sum(p, axis=0, keepdims=True))
        xt[c] = p.T.astype(BF16)
        qt[c] = row_softmax(lg).T.astype(BF16)
    pad = jnp.zeros((8 - 2 * clips, slots), F32)
    st_a[...] = jnp.concatenate(peaks + masses + [pad], axis=0)

    def combine(parts):
        m = parts[0][:clips]
        for part in parts[1:]:
            m = jnp.maximum(m, part[:clips])
        mass = None
        for part in parts:
            term = part[clips : 2 * clips] * jnp.exp(part[:clips] - m)
            mass = term if mass is None else mass + term
        return jnp.concatenate([m, mass, pad], axis=0)

    def lay_out(value, kind):
        for t in range(seq_n):
            block = value[:, t * dc : (t + 1) * dc].reshape(half, 2, owned, dc).astype(BF16)
            for q in range(2):
                buf_a[q, :, t, kind] = block[:, q]

    greet([pair] + seq_peers + exp_peers)
    copies = [net.start(st_a, st_p, pair)]
    lay_out(dot(qt[0], gout[0]), clips)
    copies[0].wait_recv()
    st_b[...] = combine([st_a[...], st_p[...]])
    copies = [net.start(st_b, st_s.at[k], peer) for k, peer in enumerate(seq_peers)]
    for c in range(1, clips):
        lay_out(dot(qt[c], gout[c]), clips + c)
    for copy in copies:
        copy.wait_recv()
    st_c[...] = combine([st_b[...]] + [st_s[k] for k in range(seq_n - 1)])
    copies = [net.start(st_c, st_z.at[k], peer) for k, peer in enumerate(exp_peers)]
    for c in range(clips):
        acc_p[c] = dot(xt[c], tok[c])
    for copy in copies:
        copy.wait_recv()
    stats = combine([st_c[...]] + [st_z[k] for k in range(half - 1)])
    scale = jnp.exp(st_a[:clips] - stats[:clips]) / stats[clips : 2 * clips]
    for c in range(clips):
        lay_out(acc_p[c] * as_column(scale[c : c + 1], slots), c)

    copy = net.start(buf_a.at[1 - par], rcv_a, pair)
    copy.wait_recv()
    for t in range(seq_n):
        buf_b[t] = (buf_a[par, :, t].astype(F32) + rcv_a[:, t].astype(F32)).astype(BF16)
    copies = [net.start(buf_b.at[peer[0]], rcv_b.at[k], peer) for k, peer in enumerate(seq_peers)]
    for copy in copies:
        copy.wait_recv()
    total = buf_b[s].astype(F32)
    for k in range(seq_n - 1):
        total = total + rcv_b[k].astype(F32)
    buf_c[...] = total.astype(BF16)
    copies = [
        net.start(buf_c.at[(h + 1 + k) % half], rcv_c.at[k], peer) for k, peer in enumerate(exp_peers)
    ]
    for copy in copies:
        copy.wait_recv()
    total = buf_c[h].astype(F32)
    for k in range(half - 1):
        total = total + rcv_c[k].astype(F32)
    xf[...] = total
    xg[s] = total.astype(BF16)
    copies = [net.start(xg.at[s], xg.at[s], peer) for peer in seq_peers]
    for copy in copies:
        copy.wait_recv()

    both = jnp.concatenate(
        [xg[t].astype(F32).reshape(kinds * owned, dc) for t in range(seq_n)], axis=1
    )
    n_rows = clips * owned
    x_rows, g_rows = both[:n_rows], both[n_rows:].astype(BF16)
    row = lax.broadcasted_iota(jnp.int32, (n_rows, 1), 0)
    expert_of = (row % owned) // (owned // experts)
    mask = [(expert_of == e).astype(F32) for e in range(experts)]
    load_in.wait()
    load_out.wait()
    pre, hidden_grad = 0.0, 0.0
    for e in range(experts):
        mine = x_rows * mask[e]
        x_o[e] = mine
        pre = pre + dot(mine.astype(BF16), win[e])
        hidden_grad = hidden_grad + dot_nt(g_rows, wout[e]) * mask[e]
    g_o[...] = g_rows
    hidden, back = jax.vjp(jax.nn.gelu, pre)
    pre_grad = back(hidden_grad)[0]
    pg_o[...] = pre_grad.astype(BF16)
    out_part, in_part = 0.0, 0.0
    for e in range(experts):
        mine = hidden * mask[e]
        hid_o[e] = mine
        out_part = out_part + dot(mine.astype(BF16), wout[e])
        in_part = in_part + dot_nt((pre_grad * mask[e]).astype(BF16), win[e])
    for t in range(seq_n):
        cut = slice(t * dc, (t + 1) * dc)
        buf_e[t, :clips] = out_part[:, cut].reshape(clips, owned, dc).astype(BF16)
        buf_e[t, clips:] = in_part[:, cut].reshape(clips, owned, dc).astype(BF16)
    copies = [net.start(buf_e.at[peer[0]], rcv_e.at[k], peer) for k, peer in enumerate(seq_peers)]
    for copy in copies:
        copy.wait_recv()
    total = buf_e[s].astype(F32)
    for k in range(seq_n - 1):
        total = total + rcv_e[k].astype(F32)
    piece = total.astype(BF16)
    ag[par, h, s] = piece
    inner = jnp.sum(piece[clips:].astype(F32) * xf[:clips], axis=2, keepdims=True)
    inn[par, h, s] = jnp.broadcast_to(inner, inn.shape[3:])

    copies = []
    for peer in exp_peers:
        copies.append(net.start(ag.at[par, h, s], ag.at[par, h, s], peer))
        copies.append(net.start(inn.at[par, h, s], inn.at[par, h, s], peer))
    for copy in copies:
        copy.wait_recv()
    copies = []
    for peer in seq_peers:
        copies.append(net.start(ag.at[par, :, s], ag.at[par, :, s], peer))
        copies.append(net.start(inn.at[par, :, s], inn.at[par, :, s], peer))
    for copy in copies:
        copy.wait_recv()
    copies = [net.start(ag.at[par], ag.at[par], pair), net.start(inn.at[par], inn.at[par], pair)]
    for copy in copies:
        copy.wait_recv()

    owners = [(q, g) for g in range(half) for q in range(2)]
    inners = []
    for c in range(clips):
        for t in range(seq_n):
            cut = slice(t * dc, (t + 1) * dc)
            for out, kind in ((so_o, c), (sg_o, clips + c)):
                out[c, :, cut] = jnp.concatenate(
                    [ag[q, g, t, kind].astype(F32) for q, g in owners], axis=0
                ).astype(BF16)
        parts = []
        for q, g in owners:
            part = inn[q, g, 0, c]
            for t in range(1, seq_n):
                part = part + inn[q, g, t, c]
            parts.append(part)
        inners.append(as_row(jnp.concatenate(parts, axis=0)[:, :1], slots))
    st_o[...] = jnp.concatenate([stats[: 2 * clips]] + inners + [jnp.zeros((8 - 3 * clips, slots), F32)], axis=0)
    net.drain()


def finish(clips, steps, tok, gout, rt, so, sg, st, x, g, hid, pg, mixed, gt, gr, gwin, gwout):
    i = pl.program_id(0)
    c = i // (steps // clips)
    peak = st[pl.ds(c, 1), :]
    mass = st[pl.ds(clips + c, 1), :]
    inner = st[pl.ds(2 * clips + c, 1), :]
    t, go = tok[0], gout[0]
    lg = dot(t, rt[...])
    dispatch = jnp.exp(lg - peak) / mass
    mixing = row_softmax(lg)
    mixing_grad = dot_nt(go, so[0])
    dispatch_grad = dot_nt(t, sg[0])
    lgrad = dispatch * (dispatch_grad - inner) + mixing * (
        mixing_grad - jnp.sum(mixing * mixing_grad, axis=1, keepdims=True)
    )
    mixed[0] = dot(mixing.astype(BF16), so[0]).astype(BF16)
    gt[0] = (dot(dispatch.astype(BF16), sg[0]) + dot_nt(lgrad.astype(BF16), rt[...])).astype(BF16)

    @pl.when(i == 0)
    def _():
        gr[...] = jnp.zeros_like(gr)

    gr[...] += dot(lgrad.T.astype(BF16), t)
    gwin[0] = dot(x[0].T.astype(BF16), pg[...]).astype(BF16)
    gwout[0] = dot(hid[0].T.astype(BF16), g[...]).astype(BF16)


def scatter(seq_n, exp_n, gr, out, buf_a, rcv_a, buf_b, rcv_b, buf_c, rcv_c, send_sem, recv_sem):
    half = exp_n // 2
    s, h, par, pair, seq_peers, exp_peers = place(seq_n, exp_n)
    rows = out.shape[0]
    net = Sender(send_sem, recv_sem)
    whole = gr[...].T
    for t in range(seq_n):
        for g in range(half):
            for q in range(2):
                at = (t * exp_n + 2 * g + q) * rows
                buf_a[q, t, g] = whole[at : at + rows]
    greet([pair] + seq_peers + exp_peers)
    net.start(buf_a.at[1 - par], rcv_a, pair).wait_recv()
    buf_b[...] = buf_a[par] + rcv_a[...]
    copies = [net.start(buf_b.at[peer[0]], rcv_b.at[k], peer) for k, peer in enumerate(seq_peers)]
    for copy in copies:
        copy.wait_recv()
    total = buf_b[s]
    for k in range(seq_n - 1):
        total = total + rcv_b[k]
    buf_c[...] = total
    copies = [
        net.start(buf_c.at[(h + 1 + k) % half], rcv_c.at[k], peer) for k, peer in enumerate(exp_peers)
    ]
    for copy in copies:
        copy.wait_recv()
    total = buf_c[h]
    for k in range(half - 1):
        total = total + rcv_c[k]
    out[...] = total
    net.drain()


def on_device(seq_n, exp_n, tokens, router, w_in, w_out, grad_out):
    clips, rows, width = tokens.shape
    slots = router.shape[1]
    experts, _, ff = w_in.shape
    half = exp_n // 2
    owned = slots // exp_n
    dc = width // seq_n
    kinds = 2 * clips
    n_rows = clips * owned
    vmem = pl.BlockSpec(memory_space=pltpu.VMEM)
    hbm = pl.BlockSpec(memory_space=pltpu.HBM)
    shape = jax.ShapeDtypeStruct
    block = (kinds, owned, dc)
    n_front = front_copies(seq_n, exp_n)
    so, sg, st, x, g, hid, pg = pl.pallas_call(
        functools.partial(front, seq_n, exp_n),
        out_shape=(
            shape((clips, slots, width), BF16),
            shape((clips, slots, width), BF16),
            shape((8, slots), F32),
            shape((experts, n_rows, width), F32),
            shape((n_rows, width), BF16),
            shape((experts, n_rows, ff), F32),
            shape((n_rows, ff), BF16),
        ),
        in_specs=[vmem, vmem, vmem, hbm, hbm],
        out_specs=(vmem,) * 7,
        scratch_shapes=[
            pltpu.VMEM(w_in.shape, BF16),
            pltpu.VMEM(w_out.shape, BF16),
            pltpu.VMEM((clips, slots, rows), BF16),
            pltpu.VMEM((clips, slots, rows), BF16),
            pltpu.VMEM((8, slots), F32),
            pltpu.VMEM((8, slots), F32),
            pltpu.VMEM((8, slots), F32),
            pltpu.VMEM((seq_n - 1, 8, slots), F32),
            pltpu.VMEM((8, slots), F32),
            pltpu.VMEM((half - 1, 8, slots), F32),
            pltpu.VMEM((2, half, seq_n) + block, BF16),
            pltpu.VMEM((half, seq_n) + block, BF16),
            pltpu.VMEM((seq_n, half) + block, BF16),
            pltpu.VMEM((seq_n - 1, half) + block, BF16),
            pltpu.VMEM((half,) + block, BF16),
            pltpu.VMEM((half - 1,) + block, BF16),
            pltpu.VMEM(block, F32),
            pltpu.VMEM((seq_n,) + block, BF16),
            pltpu.VMEM((seq_n,) + block, BF16),
            pltpu.VMEM((seq_n - 1,) + block, BF16),
            pltpu.VMEM((2, half, seq_n) + block, BF16),
            pltpu.VMEM((2, half, seq_n, clips, owned, 128), F32),
            pltpu.VMEM((clips, slots, width), F32),
            pltpu.SemaphoreType.DMA((2,)),
            pltpu.SemaphoreType.DMA((n_front,)),
            pltpu.SemaphoreType.DMA((n_front,)),
        ],
        compiler_params=pltpu.CompilerParams(collective_id=0, has_side_effects=True),
        name="front",
    )(tokens, router, grad_out, w_in, w_out)

    steps = 4 * clips
    t_blocks = steps // clips
    w_blocks = steps // experts
    token_spec = pl.BlockSpec((1, rows // t_blocks, width), lambda i: (i // t_blocks, i % t_blocks, 0))
    slot_spec = pl.BlockSpec((1, slots, width), lambda i: (i // t_blocks, 0, 0))

    def fixed(a):
        return pl.BlockSpec(a.shape, lambda i: (0,) * a.ndim)

    mixed, grad_tokens, gr, grad_w_in, grad_w_out = pl.pallas_call(
        functools.partial(finish, clips, steps),
        grid=(steps,),
        out_shape=(
            shape(tokens.shape, BF16),
            shape(tokens.shape, BF16),
            shape((slots, width), F32),
            shape(w_in.shape, BF16),
            shape(w_out.shape, BF16),
        ),
        in_specs=[
            token_spec,
            token_spec,
            fixed(router),
            slot_spec,
            slot_spec,
            fixed(st),
            pl.BlockSpec((1, n_rows, width // w_blocks), lambda i: (i // w_blocks, 0, i % w_blocks)),
            fixed(g),
            pl.BlockSpec((1, n_rows, ff // w_blocks), lambda i: (i // w_blocks, 0, i % w_blocks)),
            fixed(pg),
        ],
        out_specs=(
            token_spec,
            token_spec,
            pl.BlockSpec((slots, width), lambda i: (0, 0)),
            pl.BlockSpec((1, width // w_blocks, ff), lambda i: (i // w_blocks, i % w_blocks, 0)),
            pl.BlockSpec((1, ff // w_blocks, width), lambda i: (i // w_blocks, i % w_blocks, 0)),
        ),
        name="finish",
    )(tokens, grad_out, router, so, sg, st, x, g, hid, pg)

    out_rows = width // (seq_n * exp_n)
    n_scatter = 1 + (seq_n - 1) + (half - 1)
    tile = (out_rows, slots)
    grad_router = pl.pallas_call(
        functools.partial(scatter, seq_n, exp_n),
        out_shape=shape(tile, F32),
        in_specs=[vmem],
        out_specs=vmem,
        scratch_shapes=[
            pltpu.VMEM((2, seq_n, half) + tile, F32),
            pltpu.VMEM((seq_n, half) + tile, F32),
            pltpu.VMEM((seq_n, half) + tile, F32),
            pltpu.VMEM((seq_n - 1, half) + tile, F32),
            pltpu.VMEM((half,) + tile, F32),
            pltpu.VMEM((half - 1,) + tile, F32),
            pltpu.SemaphoreType.DMA((n_scatter,)),
            pltpu.SemaphoreType.DMA((n_scatter,)),
        ],
        compiler_params=pltpu.CompilerParams(collective_id=1, has_side_effects=True),
        name="scatter",
    )(gr)
    return mixed, grad_tokens, grad_router, grad_w_in, grad_w_out


def solution(mesh):
    return jax.shard_map(
        functools.partial(on_device, mesh.shape["seq"], mesh.shape["exp"]),
        mesh=mesh,
        in_specs=(
            P(None, ("seq", "exp"), None),
            P(),
            P("exp", None, "seq"),
            P("exp", "seq", None),
            P(None, ("seq", "exp"), None),
        ),
        out_specs=(
            P(None, ("seq", "exp"), None),
            P(None, ("seq", "exp"), None),
            P(("seq", "exp"), None),
            P("exp", None, "seq"),
            P("exp", "seq", None),
        ),
        check_vma=False,
    )
```

time: 444 us -> 80.5 us (0.18)
  blocking collectives: 200 us -> 0 us
  waiting for transfers between devices: 160 us -> 0 us
  Pallas kernels: 0 us -> 76.5 us
  matrix products: 47.6 us -> 0 us
  between operations: 14.1 us -> 0.65 us
  local copies, waits for them, and re-layouts: 16.2 us -> 3.06 us
    psum x3 -> x0, blocking collectives: 130 us -> none  [the longest x1 49.9 us: on_device(): summed = lax.psum(jnp.concatenate([inputs, grads], axis=1), ('seq', 'exp'))]
    unnamed x3 -> x0, waiting for transfers between devices: 127 us -> none
    pallas_call x0 -> x3, Pallas kernels: none -> 76.5 us  [the longest x1 48.1 us: on_device(): pl.pallas_call(functools.partial(front, seq_n, exp_n), out_shape=(shape((...]
    dot_general x15 -> x0, matrix products: 47.6 us -> none  [the longest x2 7.44 us: on_device(): jnp.einsum('cts,scd->ctd', weights, shard_rows, preferred_element_type=jn...]
    pmax x1 -> x0, blocking collectives: 41.9 us -> none  [on_device(): slot_peak = lax.pmax(jnp.max(logits, axis=1), ('seq', 'exp'))]
    psum x1 -> x0, waiting for transfers between devices: 33.1 us -> none  [on_device(): lax.psum(expert_part.astype(jnp.bfloat16), 'seq').astype(jnp.float32)]
    all_gather x2 -> x0, blocking collectives: 28.8 us -> none  [the longest x1 14.6 us: on_device(): shard_rows = lax.all_gather(slot_in_grads, 'exp', axis=0, tiled=True)]
    reshape x6 -> x0, local copies, waits for them, and re-layouts: 8.25 us -> none  [the longest x2 2.74 us: on_device(): slot_outputs = out_sums.astype(jnp.bfloat16).reshape(owned, clips, width)]
  transfers between devices with their start and end apart: 2 -> 0, of which waited for: 2 -> 0; matrix products, arithmetic and copies ran while one was open for 4% -> 0% of each run, Pallas kernels for 0% -> 0%
where the time goes in v1:
time: 80.5 us; the launch traced here: 80.2 us
  Pallas kernels  76.5 us (95%)
  local copies, waits for them, and re-layouts  3.06 us (4%)
    pallas_call x1, Pallas kernels, on_device(): pl.pallas_call(functools.partial(front, seq_n, exp_n), out_shape=(shape((...  48.1 us
    pallas_call x1, Pallas kernels, on_device(): pl.pallas_call(functools.partial(scatter, seq_n, exp_n), out_shape=shape(...  14.5 us
    pallas_call x1, Pallas kernels, on_device(): pl.pallas_call(functools.partial(finish, clips, steps), grid=(steps,), ou...  13.9 us
    unnamed x2, local copies, waits for them, and re-layouts  3.06 us

profile of v1, /device:TPU:0, one launch (start us, length us, event | category | flops | bytes accessed | tf_op | source)
XLA Modules:
  0.0 80.2 jit_solution(2500761015033822716)
XLA Ops:
  0.6 1.7 %copy.11.rt = bf16[1024,64]{1,0:T(8,128)(2,1)} copy(bf16[1024,64]{0,1:T(8,128)(2,1)} %param.6) | data formatting | bytes 262144 | tf_op args[1]
  2.4 48.1 %front.1 = (bf16[2,64,1024]{2,1,0:T(8,128)(2,1)}, bf16[2,64,1024]{2,1,0:T(8,128)(2,1)}, f32[8,64]{1,0:T(8,128)}, f32[2,16,1024]{2,1,0:T(8,128)}, bf16[16,1024]{1...) custom-call(bf16[2,768,1024]{2,1,0:T(8,128)(2,1)} %tok.3, bf16[1024,64]{1,0:T(8,128)(2,1)} %copy.11.rt, ...), custom_call_target="tpu_custom_call" | custom-call | tf_op jit(solution)/shard_map/front/pallas_call | solution.py:335
  50.5 13.9 %finish.1 = (bf16[2,768,1024]{2,1,0:T(8,128)(2,1)}, bf16[2,768,1024]{2,1,0:T(8,128)(2,1)}, f32[64,1024]{1,0:T(8,128)}, bf16[2,1024,1024]{2,1,0:T(8,128)(2,1)}, bf16[2,1024,1024]{2,1,0:T(8,128)(2,1)}) custom-call(bf16[2,768,1024]{2,1,0:T(8,128)(2,1)} %tok.3, bf16[2,768,1024]{2,1,0:T(8,128)(2,1)} %gout.3, bf16[1024,64]{1,0:T(8,128)(2,1)} %copy.11.rt, ...), custom_call_target="tpu_custom_call" | custom-call | tf_op jit(solution)/shard_map/finish/pallas_call | solution.py:389
  64.3 14.5 %scatter.1 = f32[32,64]{1,0:T(8,128)} custom-call(f32[64,1024]{1,0:T(8,128)} %get-tuple-element.26.gr), custom_call_target="tpu_custom_call" | custom-call | tf_op jit(solution)/shard_map/scatter/pallas_call | solution.py:424
  78.9 1.3 %copy.13 = f32[32,64]{1,0:T(8,128)} copy(f32[32,64]{1,0:T(8,128)} %scatter.1) | data formatting | bytes 16384

commit v2 on v1

v2 whole, which is shorter than its diff:
```python
import functools

import jax
import jax.numpy as jnp
from jax import lax
from jax.experimental import pallas as pl
from jax.experimental.pallas import tpu as pltpu
from jax.sharding import PartitionSpec as P

MESH = pl.DeviceIdType.MESH
F32 = jnp.float32
BF16 = jnp.bfloat16
NT = (((1,), (1,)), ((), ()))


def dot(a, b):
    return jnp.dot(a, b, preferred_element_type=F32)


def dot_nt(a, b):
    return lax.dot_general(a, b, NT, preferred_element_type=F32)


def place(seq_n, exp_n):
    s = lax.axis_index("seq")
    e = lax.axis_index("exp")
    h, par = e // 2, e % 2
    pair = (s, h * 2 + (1 - par))
    seq_peers = [((s + k) % seq_n, e) for k in range(1, seq_n)]
    exp_peers = [(s, ((h + k) % (exp_n // 2)) * 2 + par) for k in range(1, exp_n // 2)]
    return s, h, par, pair, seq_peers, exp_peers


def greet(peers):
    barrier = pltpu.get_barrier_semaphore()
    for peer in peers:
        pl.semaphore_signal(barrier, inc=1, device_id=peer, device_id_type=MESH)


def await_greetings(peers):
    pl.semaphore_wait(pltpu.get_barrier_semaphore(), len(peers))


class Sender:
    def __init__(self, send_sem, recv_sem):
        self.send_sem, self.recv_sem, self.count, self.open = send_sem, recv_sem, 0, []

    def start(self, src, dst, peer):
        copy = pltpu.make_async_remote_copy(
            src_ref=src,
            dst_ref=dst,
            send_sem=self.send_sem.at[self.count],
            recv_sem=self.recv_sem.at[self.count],
            device_id=peer,
            device_id_type=MESH,
        )
        copy.start()
        self.count += 1
        self.open.append(copy)
        return copy

    def drain(self):
        for copy in self.open:
            copy.wait_send()


def front_copies(seq_n, exp_n):
    seq, rest = seq_n - 1, exp_n // 2 - 1
    gather = 1 + seq + rest
    return gather + 2 * (gather + seq) + 2 * seq + 3 * gather


def as_column(row, n):
    eye = lax.broadcasted_iota(jnp.int32, (n, n), 0) == lax.broadcasted_iota(jnp.int32, (n, n), 1)
    return jnp.sum(jnp.where(eye, jnp.broadcast_to(row, (n, n)), 0.0), axis=1, keepdims=True)


def as_row(column, n):
    eye = lax.broadcasted_iota(jnp.int32, (n, n), 0) == lax.broadcasted_iota(jnp.int32, (n, n), 1)
    return jnp.sum(jnp.where(eye, jnp.broadcast_to(column, (n, n)), 0.0), axis=0, keepdims=True)


def row_softmax(lg):
    q = jnp.exp(lg - jnp.max(lg, axis=1, keepdims=True))
    return q / jnp.sum(q, axis=1, keepdims=True)


def front(
    seq_n, exp_n, tok_hbm, rt, gout_hbm, win_hbm, wout_hbm,
    so_o, wr_o, st_o, x_o, g_o, hid_o, pg_o,
    tok, gout, win, wout, xt, qt, st_a, st_p, st_b, st_s, st_c, st_z,
    buf_a, rcv_a, buf_b, rcv_b, buf_c, rcv_c, xf, xg, buf_e, rcv_e, ag, inn, acc_p,
    w_sem, send_sem, recv_sem,
):
    clips, rows, width = tok.shape
    slots = rt.shape[0]
    half = exp_n // 2
    owned = slots // exp_n
    dc = width // seq_n
    n_rows = clips * owned
    experts = win.shape[0]
    s, h, par, pair, seq_peers, exp_peers = place(seq_n, exp_n)

    load_tok = [pltpu.make_async_copy(tok_hbm.at[c], tok.at[c], w_sem.at[c]) for c in range(clips)]
    load_gout = [
        pltpu.make_async_copy(gout_hbm.at[c], gout.at[c], w_sem.at[clips + c]) for c in range(clips)
    ]
    load_in = pltpu.make_async_copy(win_hbm, win, w_sem.at[2 * clips])
    load_out = pltpu.make_async_copy(wout_hbm, wout, w_sem.at[2 * clips + 1])
    for load in load_tok + load_gout:
        load.start()
    greet([pair] + seq_peers + exp_peers)
    net = Sender(send_sem, recv_sem)

    peaks, masses = [], []
    for c in range(clips):
        load_tok[c].wait()
        if c == clips - 1:
            load_out.start()
            load_in.start()
        lg = dot_nt(tok[c], rt[...])
        m = jnp.max(lg, axis=0, keepdims=True)
        p = jnp.exp(lg - m)
        peaks.append(m)
        masses.append(jnp.sum(p, axis=0, keepdims=True))
        xt[c] = p.T.astype(BF16)
        qt[c] = row_softmax(lg).T.astype(BF16)
    pad = jnp.zeros((8 - 2 * clips, slots), F32)
    st_a[...] = jnp.concatenate(peaks + masses + [pad], axis=0)

    def combine(parts):
        m = parts[0][:clips]
        for part in parts[1:]:
            m = jnp.maximum(m, part[:clips])
        mass = None
        for part in parts:
            term = part[clips : 2 * clips] * jnp.exp(part[:clips] - m)
            mass = term if mass is None else mass + term
        return jnp.concatenate([m, mass, pad], axis=0)

    def lay_out(value, kind, c):
        for t in range(seq_n):
            block = value[:, t * dc : (t + 1) * dc].reshape(half, 2, owned, dc).astype(BF16)
            for q in range(2):
                buf_a[kind, q, :, t, c] = block[:, q]

    def arrived(copies):
        for copy in copies:
            copy.wait_recv()

    def total_of(own, parts, count):
        total = own.astype(F32)
        for k in range(count):
            total = total + parts[k].astype(F32)
        return total

    def to_pair(kind):
        return [net.start(buf_a.at[kind, 1 - par], rcv_a.at[kind], pair)]

    def to_seq(kind):
        for t in range(seq_n):
            mine = buf_a[kind, par, :, t].astype(F32)
            buf_b[kind, t] = (mine + rcv_a[kind, :, t].astype(F32)).astype(BF16)
        return [
            net.start(buf_b.at[kind, peer[0]], rcv_b.at[kind, k], peer)
            for k, peer in enumerate(seq_peers)
        ]

    def to_exp(kind):
        buf_c[kind] = total_of(buf_b[kind, s], rcv_b.at[kind], seq_n - 1).astype(BF16)
        return [
            net.start(buf_c.at[kind, (h + 1 + k) % half], rcv_c.at[kind, k], peer)
            for k, peer in enumerate(exp_peers)
        ]

    def to_group(kind):
        total = total_of(buf_c[kind, h], rcv_c.at[kind], half - 1)
        if kind == 0:
            xf[...] = total
        xg[kind, s] = total.astype(BF16)
        return [net.start(xg.at[kind, s], xg.at[kind, s], peer) for peer in seq_peers]

    def rows_of(kind):
        return jnp.concatenate(
            [xg[kind, t].astype(F32).reshape(n_rows, dc) for t in range(seq_n)], axis=1
        )

    await_greetings([pair] + seq_peers + exp_peers)
    stat = [net.start(st_a, st_p, pair)]
    load_gout[0].wait()
    lay_out(dot(qt[0], gout[0]), 1, 0)
    arrived(stat)
    st_b[...] = combine([st_a[...], st_p[...]])
    stat = [net.start(st_b, st_s.at[k], peer) for k, peer in enumerate(seq_peers)]
    for c in range(1, clips):
        load_gout[c].wait()
        lay_out(dot(qt[c], gout[c]), 1, c)
    grads = to_pair(1)
    arrived(stat)
    st_c[...] = combine([st_b[...]] + [st_s[k] for k in range(seq_n - 1)])
    stat = [net.start(st_c, st_z.at[k], peer) for k, peer in enumerate(exp_peers)]
    for c in range(clips):
        acc_p[c] = dot(xt[c], tok[c])
        if c == 0:
            arrived(grads)
            grads = to_seq(1)
    arrived(stat)
    stats = combine([st_c[...]] + [st_z[k] for k in range(half - 1)])
    scale = jnp.exp(st_a[:clips] - stats[:clips]) / stats[clips : 2 * clips]
    for c in range(clips):
        lay_out(acc_p[c] * as_column(scale[c : c + 1], slots), 0, c)
    inputs = to_pair(0)
    arrived(grads)
    grads = to_exp(1)
    arrived(inputs)
    inputs = to_seq(0)
    arrived(grads)
    grads = to_group(1)
    arrived(inputs)
    inputs = to_exp(0)
    arrived(grads)

    row = lax.broadcasted_iota(jnp.int32, (n_rows, 1), 0)
    expert_of = (row % owned) // (owned // experts)
    mask = [(expert_of == e).astype(F32) for e in range(experts)]
    g_rows = rows_of(1).astype(BF16)
    g_o[...] = g_rows
    load_out.wait()
    hidden_grad = 0.0
    for e in range(experts):
        hidden_grad = hidden_grad + dot_nt(g_rows, wout[e]) * mask[e]
    load_in.wait()

    arrived(inputs)
    inputs = to_group(0)
    arrived(inputs)
    x_rows = rows_of(0)
    pre = 0.0
    for e in range(experts):
        mine = x_rows * mask[e]
        x_o[e] = mine
        pre = pre + dot(mine.astype(BF16), win[e])
    hidden, back = jax.vjp(jax.nn.gelu, pre)
    pre_grad = back(hidden_grad)[0]

    def share(kind, part):
        for t in range(seq_n):
            cut = slice(t * dc, (t + 1) * dc)
            buf_e[kind, t] = part[:, cut].reshape(clips, owned, dc).astype(BF16)
        return [
            net.start(buf_e.at[kind, peer[0]], rcv_e.at[kind, k], peer)
            for k, peer in enumerate(seq_peers)
        ]

    in_part = 0.0
    for e in range(experts):
        in_part = in_part + dot_nt((pre_grad * mask[e]).astype(BF16), win[e])
    backward = share(1, in_part)
    out_part = 0.0
    for e in range(experts):
        mine = hidden * mask[e]
        hid_o[e] = mine
        out_part = out_part + dot(mine.astype(BF16), wout[e])
    forward = share(0, out_part)
    pg_o[...] = pre_grad.astype(BF16)

    def gather_exp(kind):
        piece = total_of(buf_e[kind, s], rcv_e.at[kind], seq_n - 1).astype(BF16)
        ag[kind, par, h, s] = piece
        copies = []
        if kind == 1:
            inner = jnp.sum(piece.astype(F32) * xf[...], axis=2, keepdims=True)
            lane = lax.broadcasted_iota(jnp.int32, inn.shape[3:], 1)
            tile = jnp.zeros(inn.shape[3:], F32)
            for c in range(clips):
                tile = jnp.where(lane == c, inner[c], tile)
            inn[par, h, s] = tile
            for peer in exp_peers:
                copies.append(net.start(inn.at[par, h, s], inn.at[par, h, s], peer))
        for peer in exp_peers:
            copies.append(net.start(ag.at[kind, par, h, s], ag.at[kind, par, h, s], peer))
        return copies

    def gather_seq(kind):
        copies = []
        for peer in seq_peers:
            if kind == 1:
                copies.append(net.start(inn.at[par, :, s], inn.at[par, :, s], peer))
            copies.append(net.start(ag.at[kind, par, :, s], ag.at[kind, par, :, s], peer))
        return copies

    def gather_pair(kind):
        copies = [net.start(ag.at[kind, par], ag.at[kind, par], pair)]
        if kind == 1:
            copies.append(net.start(inn.at[par], inn.at[par], pair))
        return copies

    owners = [(q, g) for g in range(half) for q in range(2)]

    def write_out(kind):
        for c in range(clips):
            for t in range(seq_n):
                cut = slice(t * dc, (t + 1) * dc)
                value = jnp.concatenate(
                    [ag[kind, q, g, t, c].astype(F32) for q, g in owners], axis=0
                ).astype(BF16)
                if kind == 0:
                    so_o[c, :, cut] = value
                else:
                    wr_o[c, slots:, cut] = value

    arrived(backward)
    backward = gather_exp(1)
    arrived(forward)
    forward = gather_exp(0)
    for c in range(clips):
        wr_o[c, :slots] = rt[...]
    arrived(backward)
    backward = gather_seq(1)
    arrived(forward)
    forward = gather_seq(0)
    arrived(backward)
    backward = gather_pair(1)
    arrived(forward)
    forward = gather_pair(0)
    arrived(backward)
    write_out(1)
    parts = []
    for q, g in owners:
        part = inn[q, g, 0]
        for t in range(1, seq_n):
            part = part + inn[q, g, t]
        parts.append(part)
    inners = jnp.concatenate(parts, axis=0)
    inners = [as_row(inners[:, c : c + 1], slots) for c in range(clips)]
    st_o[...] = jnp.concatenate(
        [stats[: 2 * clips]] + inners + [jnp.zeros((8 - 3 * clips, slots), F32)], axis=0
    )
    arrived(forward)
    write_out(0)
    net.drain()


def finish(clips, steps, tok, gout, so, wr, st, x, g, hid, pg, mixed, gt, gr, gwin, gwout):
    i = pl.program_id(0)
    c = i // (steps // clips)
    slots = so.shape[1]
    peak = st[pl.ds(c, 1), :]
    mass = st[pl.ds(clips + c, 1), :]
    inner = st[pl.ds(2 * clips + c, 1), :]
    t, go = tok[0], gout[0]
    both = dot_nt(t, wr[0])
    lg, dispatch_grad = both[:, :slots], both[:, slots:]
    mixing_grad = dot_nt(go, so[0])
    dispatch = jnp.exp(lg - peak) / mass
    mixing = row_softmax(lg)
    lgrad = dispatch * (dispatch_grad - inner) + mixing * (
        mixing_grad - jnp.sum(mixing * mixing_grad, axis=1, keepdims=True)
    )
    mixed[0] = dot(mixing.astype(BF16), so[0]).astype(BF16)
    gt[0] = dot(jnp.concatenate([lgrad, dispatch], axis=1).astype(BF16), wr[0]).astype(BF16)

    @pl.when(i == 0)
    def _():
        gr[...] = jnp.zeros_like(gr)

    gr[...] += dot(lgrad.T.astype(BF16), t)
    gwin[0] = dot(x[0].T.astype(BF16), pg[...]).astype(BF16)
    gwout[0] = dot(hid[0].T.astype(BF16), g[...]).astype(BF16)


def scatter(seq_n, exp_n, gr, out, buf_a, rcv_a, buf_b, rcv_b, buf_c, rcv_c, send_sem, recv_sem):
    half = exp_n // 2
    s, h, par, pair, seq_peers, exp_peers = place(seq_n, exp_n)
    rows, slots = out.shape
    packed = buf_c.shape[1]
    pack = rows // packed
    greet([pair] + seq_peers + exp_peers)
    net = Sender(send_sem, recv_sem)
    whole = gr[...].T
    for t in range(seq_n):
        for g in range(half):
            for q in range(2):
                at = (t * exp_n + 2 * g + q) * rows
                parts = [whole[at + j * packed : at + (j + 1) * packed] for j in range(pack)]
                buf_a[q, t, g] = jnp.concatenate(parts, axis=1).astype(BF16)
    await_greetings([pair] + seq_peers + exp_peers)
    net.start(buf_a.at[1 - par], rcv_a, pair).wait_recv()
    buf_b[...] = (buf_a[par].astype(F32) + rcv_a[...].astype(F32)).astype(BF16)
    copies = [net.start(buf_b.at[peer[0]], rcv_b.at[k], peer) for k, peer in enumerate(seq_peers)]
    for copy in copies:
        copy.wait_recv()
    total = buf_b[s].astype(F32)
    for k in range(seq_n - 1):
        total = total + rcv_b[k].astype(F32)
    buf_c[...] = total.astype(BF16)
    copies = [
        net.start(buf_c.at[(h + 1 + k) % half], rcv_c.at[k], peer) for k, peer in enumerate(exp_peers)
    ]
    for copy in copies:
        copy.wait_recv()
    total = buf_c[h].astype(F32)
    for k in range(half - 1):
        total = total + rcv_c[k].astype(F32)
    for j in range(pack):
        out[j * packed : (j + 1) * packed] = total[:, j * slots : (j + 1) * slots]
    net.drain()


def on_device(seq_n, exp_n, tokens, router, w_in, w_out, grad_out):
    clips, rows, width = tokens.shape
    slots = router.shape[1]
    experts, _, ff = w_in.shape
    half = exp_n // 2
    owned = slots // exp_n
    dc = width // seq_n
    n_rows = clips * owned
    router_t = router.T
    vmem = pl.BlockSpec(memory_space=pltpu.VMEM)
    hbm = pl.BlockSpec(memory_space=pltpu.HBM)
    shape = jax.ShapeDtypeStruct
    block = (clips, owned, dc)
    n_front = front_copies(seq_n, exp_n)
    so, wr, st, x, g, hid, pg = pl.pallas_call(
        functools.partial(front, seq_n, exp_n),
        out_shape=(
            shape((clips, slots, width), BF16),
            shape((clips, 2 * slots, width), BF16),
            shape((8, slots), F32),
            shape((experts, n_rows, width), F32),
            shape((n_rows, width), BF16),
            shape((experts, n_rows, ff), F32),
            shape((n_rows, ff), BF16),
        ),
        in_specs=[hbm, vmem, hbm, hbm, hbm],
        out_specs=(vmem,) * 7,
        scratch_shapes=[
            pltpu.VMEM(tokens.shape, BF16),
            pltpu.VMEM(tokens.shape, BF16),
            pltpu.VMEM(w_in.shape, BF16),
            pltpu.VMEM(w_out.shape, BF16),
            pltpu.VMEM((clips, slots, rows), BF16),
            pltpu.VMEM((clips, slots, rows), BF16),
            pltpu.VMEM((8, slots), F32),
            pltpu.VMEM((8, slots), F32),
            pltpu.VMEM((8, slots), F32),
            pltpu.VMEM((seq_n - 1, 8, slots), F32),
            pltpu.VMEM((8, slots), F32),
            pltpu.VMEM((half - 1, 8, slots), F32),
            pltpu.VMEM((2, 2, half, seq_n) + block, BF16),
            pltpu.VMEM((2, half, seq_n) + block, BF16),
            pltpu.VMEM((2, seq_n, half) + block, BF16),
            pltpu.VMEM((2, seq_n - 1, half) + block, BF16),
            pltpu.VMEM((2, half) + block, BF16),
            pltpu.VMEM((2, half - 1) + block, BF16),
            pltpu.VMEM(block, F32),
            pltpu.VMEM((2, seq_n) + block, BF16),
            pltpu.VMEM((2, seq_n) + block, BF16),
            pltpu.VMEM((2, seq_n - 1) + block, BF16),
            pltpu.VMEM((2, 2, half, seq_n) + block, BF16),
            pltpu.VMEM((2, half, seq_n, owned, 128), F32),
            pltpu.VMEM((clips, slots, width), F32),
            pltpu.SemaphoreType.DMA((2 * clips + 2,)),
            pltpu.SemaphoreType.DMA((n_front,)),
            pltpu.SemaphoreType.DMA((n_front,)),
        ],
        compiler_params=pltpu.CompilerParams(collective_id=0, has_side_effects=True),
        name="front",
    )(tokens, router_t, grad_out, w_in, w_out)

    steps = 4 * clips
    t_blocks = steps // clips
    w_blocks = steps // experts
    token_spec = pl.BlockSpec((1, rows // t_blocks, width), lambda i: (i // t_blocks, i % t_blocks, 0))

    def slot_spec(a):
        return pl.BlockSpec((1,) + a.shape[1:], lambda i: (i // t_blocks, 0, 0))

    def fixed(a):
        return pl.BlockSpec(a.shape, lambda i: (0,) * a.ndim)

    mixed, grad_tokens, gr, grad_w_in, grad_w_out = pl.pallas_call(
        functools.partial(finish, clips, steps),
        grid=(steps,),
        out_shape=(
            shape(tokens.shape, BF16),
            shape(tokens.shape, BF16),
            shape((slots, width), F32),
            shape(w_in.shape, BF16),
            shape(w_out.shape, BF16),
        ),
        in_specs=[
            token_spec,
            token_spec,
            slot_spec(so),
            slot_spec(wr),
            fixed(st),
            pl.BlockSpec((1, n_rows, width // w_blocks), lambda i: (i // w_blocks, 0, i % w_blocks)),
            fixed(g),
            pl.BlockSpec((1, n_rows, ff // w_blocks), lambda i: (i // w_blocks, 0, i % w_blocks)),
            fixed(pg),
        ],
        out_specs=(
            token_spec,
            token_spec,
            pl.BlockSpec((slots, width), lambda i: (0, 0)),
            pl.BlockSpec((1, width // w_blocks, ff), lambda i: (i // w_blocks, i % w_blocks, 0)),
            pl.BlockSpec((1, ff // w_blocks, width), lambda i: (i // w_blocks, i % w_blocks, 0)),
        ),
        name="finish",
    )(tokens, grad_out, so, wr, st, x, g, hid, pg)

    out_rows = width // (seq_n * exp_n)
    n_scatter = 1 + (seq_n - 1) + (half - 1)
    pack = max(1, 128 // slots)
    tile = (out_rows // pack, slots * pack)
    grad_router = pl.pallas_call(
        functools.partial(scatter, seq_n, exp_n),
        out_shape=shape((out_rows, slots), F32),
        in_specs=[vmem],
        out_specs=vmem,
        scratch_shapes=[
            pltpu.VMEM((2, seq_n, half) + tile, BF16),
            pltpu.VMEM((seq_n, half) + tile, BF16),
            pltpu.VMEM((seq_n, half) + tile, BF16),
            pltpu.VMEM((seq_n - 1, half) + tile, BF16),
            pltpu.VMEM((half,) + tile, BF16),
            pltpu.VMEM((half - 1,) + tile, BF16),
            pltpu.SemaphoreType.DMA((n_scatter,)),
            pltpu.SemaphoreType.DMA((n_scatter,)),
        ],
        compiler_params=pltpu.CompilerParams(collective_id=1, has_side_effects=True),
        name="scatter",
    )(gr)
    return mixed, grad_tokens, grad_router, grad_w_in, grad_w_out


def solution(mesh):
    return jax.shard_map(
        functools.partial(on_device, mesh.shape["seq"], mesh.shape["exp"]),
        mesh=mesh,
        in_specs=(
            P(None, ("seq", "exp"), None),
            P(),
            P("exp", None, "seq"),
            P("exp", "seq", None),
            P(None, ("seq", "exp"), None),
        ),
        out_specs=(
            P(None, ("seq", "exp"), None),
            P(None, ("seq", "exp"), None),
            P(("seq", "exp"), None),
            P("exp", None, "seq"),
            P("exp", "seq", None),
        ),
        check_vma=False,
    )
```

time: 80.5 us -> 71.9 us (0.89)
  Pallas kernels: 76.5 us -> 69.7 us
  local copies, waits for them, and re-layouts: 3.06 us -> 1.32 us
    pallas_call x1, Pallas kernels: 48.1 us -> 43.8 us  [on_device(): pl.pallas_call(functools.partial(front, seq_n, exp_n), out_shape=(shape((...]
    pallas_call x1, Pallas kernels: 14.5 us -> 11.1 us  [on_device(): pl.pallas_call(functools.partial(scatter, seq_n, exp_n), out_shape=shape(...]
    unnamed x2 -> x1, local copies, waits for them, and re-layouts: 3.06 us -> 1.32 us
    pallas_call x1, Pallas kernels: 13.9 us -> 14.8 us  [on_device(): pl.pallas_call(functools.partial(finish, clips, steps), grid=(steps,), ou...]
where the time goes in v2:
time: 71.9 us; the launch traced here: 71.7 us
  Pallas kernels  69.7 us (97%)
  local copies, waits for them, and re-layouts  1.32 us (2%)
    pallas_call x1, Pallas kernels, on_device(): pl.pallas_call(functools.partial(front, seq_n, exp_n), out_shape=(shape((...  43.8 us
    pallas_call x1, Pallas kernels, on_device(): pl.pallas_call(functools.partial(finish, clips, steps), grid=(steps,), ou...  14.8 us
    pallas_call x1, Pallas kernels, on_device(): pl.pallas_call(functools.partial(scatter, seq_n, exp_n), out_shape=shape(...  11.1 us

profile of v2, /device:TPU:0, one launch (start us, length us, event | category | flops | bytes accessed | tf_op | source)
XLA Modules:
  0.0 71.7 jit_solution(2391298399275300549)
XLA Ops:
  0.6 43.8 %front.1 = (bf16[2,64,1024]{2,1,0:T(8,128)(2,1)}, bf16[2,128,1024]{2,1,0:T(8,128)(2,1)}, f32[8,64]{1,0:T(8,128)}, f32[2,16,1024]{2,1,0:T(8,128)}, bf16[16,1024]{...) custom-call(bf16[2,768,1024]{2,1,0:T(8,128)(2,1)} %tok.1, bf16[64,1024]{1,0:T(8,128)(2,1)} %bitcast.1, ...), custom_call_target="tpu_custom_call" | custom-call | tf_op jit(solution)/shard_map/front/pallas_call | solution.py:424
  44.5 14.8 %finish.1 = (bf16[2,768,1024]{2,1,0:T(8,128)(2,1)}, bf16[2,768,1024]{2,1,0:T(8,128)(2,1)}, f32[64,1024]{1,0:T(8,128)}, bf16[2,1024,1024]{2,1,0:T(8,128)(2,1)}, bf16[2,1024,1024]{2,1,0:T(8,128)(2,1)}) custom-call(bf16[2,768,1024]{2,1,0:T(8,128)(2,1)} %tok.1, bf16[2,768,1024]{2,1,0:T(8,128)(2,1)} %gout.1, bf16[2,64,1024]{2,1,0:T(8,128)(2,1)} %get-tuple-element.17.so, ...), custom_call_target="tpu_custom_call" | custom-call | tf_op jit(solution)/shard_map/finish/pallas_call | solution.py:482
  59.2 11.1 %scatter.1 = f32[32,64]{1,0:T(8,128)} custom-call(f32[64,1024]{1,0:T(8,128)} %get-tuple-element.26.gr), custom_call_target="tpu_custom_call" | custom-call | tf_op jit(solution)/shard_map/scatter/pallas_call | solution.py:517
  70.4 1.3 %copy.11 = f32[32,64]{1,0:T(8,128)} copy(f32[32,64]{1,0:T(8,128)} %scatter.1) | data formatting | bytes 16384

commit v3 on v2

--- a/solution.py
+++ b/solution.py
@@ -65,14 +65,11 @@
 
 
 def front_copies(seq_n, exp_n):
-    seq, rest = seq_n - 1, exp_n // 2 - 1
-    gather = 1 + seq + rest
-    return gather + 2 * (gather + seq) + 2 * seq + 3 * gather
-
-
-def as_column(row, n):
-    eye = lax.broadcasted_iota(jnp.int32, (n, n), 0) == lax.broadcasted_iota(jnp.int32, (n, n), 1)
-    return jnp.sum(jnp.where(eye, jnp.broadcast_to(row, (n, n)), 0.0), axis=1, keepdims=True)
+    half = exp_n // 2
+    seq, rest = seq_n - 1, half - 1
+    stats = 1 + seq + rest
+    gather = rest + half * seq + seq_n
+    return stats + 2 * (stats + seq) + 2 * seq + 3 * gather
 
 
 def as_row(column, n):
@@ -89,7 +86,7 @@
     seq_n, exp_n, tok_hbm, rt, gout_hbm, win_hbm, wout_hbm,
     so_o, wr_o, st_o, x_o, g_o, hid_o, pg_o,
     tok, gout, win, wout, xt, qt, st_a, st_p, st_b, st_s, st_c, st_z,
-    buf_a, rcv_a, buf_b, rcv_b, buf_c, rcv_c, xf, xg, buf_e, rcv_e, ag, inn, acc_p,
+    buf_a, rcv_a, buf_b, rcv_b, buf_c, rcv_c, xf, xg, buf_e, rcv_e, ag, inn, fac_a, fac_b, fac_c,
     w_sem, send_sem, recv_sem,
 ):
     clips, rows, width = tok.shape
@@ -157,27 +154,72 @@
     def to_pair(kind):
         return [net.start(buf_a.at[kind, 1 - par], rcv_a.at[kind], pair)]
 
+    def factors(ref, tiles, joint, norm=None):
+        terms = [jnp.exp(tile[:clips] - joint[:clips]) for tile in tiles]
+        if norm is not None:
+            terms = [term / norm for term in terms]
+        spare = ref.shape[3] - clips * len(tiles)
+        if spare:
+            terms.append(jnp.zeros((spare, slots), F32))
+        columns = jnp.concatenate(terms, axis=0).T.reshape(half, 2, owned, ref.shape[3])
+        for q in range(2):
+            ref[q] = columns[:, q]
+
     def to_seq(kind):
+        if kind == 0:
+            factors(fac_a, [st_a[...], st_p[...]], st_b[...])
+            fac = fac_a[par]
         for t in range(seq_n):
-            mine = buf_a[kind, par, :, t].astype(F32)
-            buf_b[kind, t] = (mine + rcv_a[kind, :, t].astype(F32)).astype(BF16)
+            for c in range(clips):
+                mine = buf_a[kind, par, :, t, c].astype(F32)
+                other = rcv_a[kind, :, t, c].astype(F32)
+                if kind == 0:
+                    mine = mine * fac[:, :, c : c + 1]
+                    other = other * fac[:, :, clips + c : clips + c + 1]
+                buf_b[kind, t, :, c] = (mine + other).astype(BF16)
         return [
             net.start(buf_b.at[kind, peer[0]], rcv_b.at[kind, k], peer)
             for k, peer in enumerate(seq_peers)
         ]
 
     def to_exp(kind):
-        buf_c[kind] = total_of(buf_b[kind, s], rcv_b.at[kind], seq_n - 1).astype(BF16)
+        if kind == 0:
+            factors(fac_b, [st_b[...]] + [st_s[k] for k in range(seq_n - 1)], st_c[...])
+            fac = fac_b[par]
+        for c in range(clips):
+            total = buf_b[kind, s, :, c].astype(F32)
+            if kind == 0:
+                total = total * fac[:, :, c : c + 1]
+            for k in range(seq_n - 1):
+                part = rcv_b[kind, k, :, c].astype(F32)
+                if kind == 0:
+                    at = (k + 1) * clips + c
+                    part = part * fac[:, :, at : at + 1]
+                total = total + part
+            buf_c[kind, :, c] = total.astype(BF16)
         return [
             net.start(buf_c.at[kind, (h + 1 + k) % half], rcv_c.at[kind, k], peer)
             for k, peer in enumerate(exp_peers)
         ]
 
     def to_group(kind):
-        total = total_of(buf_c[kind, h], rcv_c.at[kind], half - 1)
         if kind == 0:
-            xf[...] = total
-        xg[kind, s] = total.astype(BF16)
+            tiles = [st_c[...]] + [st_z[k] for k in range(half - 1)]
+            factors(fac_c, tiles, stats, stats[clips : 2 * clips])
+            fac = fac_c[par, h]
+        for c in range(clips):
+            total = buf_c[kind, h, c].astype(F32)
+            if kind == 0:
+                total = total * fac[:, c : c + 1]
+            for k in range(half - 1):
+                part = rcv_c[kind, k, c].astype(F32)
+                if kind == 0:
+                    at = (k + 1) * clips + c
+                    part = part * fac[:, at : at + 1]
+                total = total + part
+            if kind == 0:
+                xf[c] = total
+            xg[kind, s, c] = total.astype(BF16)
         return [net.start(xg.at[kind, s], xg.at[kind, s], peer) for peer in seq_peers]
 
     def rows_of(kind):
@@ -187,11 +229,16 @@
 
     await_greetings([pair] + seq_peers + exp_peers)
     stat = [net.start(st_a, st_p, pair)]
+    for c in range(clips):
+        lay_out(dot(xt[c], tok[c]), 0, c)
+    inputs = to_pair(0)
     load_gout[0].wait()
     lay_out(dot(qt[0], gout[0]), 1, 0)
     arrived(stat)
     st_b[...] = combine([st_a[...], st_p[...]])
     stat = [net.start(st_b, st_s.at[k], peer) for k, peer in enumerate(seq_peers)]
+    arrived(inputs)
+    inputs = to_seq(0)
     for c in range(1, clips):
         load_gout[c].wait()
         lay_out(dot(qt[c], gout[c]), 1, c)
@@ -199,40 +246,24 @@
     arrived(stat)
     st_c[...] = combine([st_b[...]] + [st_s[k] for k in range(seq_n - 1)])
     stat = [net.start(st_c, st_z.at[k], peer) for k, peer in enumerate(exp_peers)]
-    for c in range(clips):
-        acc_p[c] = dot(xt[c], tok[c])
-        if c == 0:
-            arrived(grads)
-            grads = to_seq(1)
-    arrived(stat)
-    stats = combine([st_c[...]] + [st_z[k] for k in range(half - 1)])
-    scale = jnp.exp(st_a[:clips] - stats[:clips]) / stats[clips : 2 * clips]
-    for c in range(clips):
-        lay_out(acc_p[c] * as_column(scale[c : c + 1], slots), 0, c)
-    inputs = to_pair(0)
     arrived(grads)
-    grads = to_exp(1)
-    arrived(inputs)
-    inputs = to_seq(0)
-    arrived(grads)
-    grads = to_group(1)
+    grads = to_seq(1)
     arrived(inputs)
     inputs = to_exp(0)
     arrived(grads)
+    grads = to_exp(1)
+    arrived(stat)
+    stats = combine([st_c[...]] + [st_z[k] for k in range(half - 1)])
+    arrived(inputs)
+    inputs = to_group(0)
+    arrived(grads)
+    grads = to_group(1)
 
     row = lax.broadcasted_iota(jnp.int32, (n_rows, 1), 0)
     expert_of = (row % owned) // (owned // experts)
     mask = [(expert_of == e).astype(F32) for e in range(experts)]
-    g_rows = rows_of(1).astype(BF16)
-    g_o[...] = g_rows
     load_out.wait()
-    hidden_grad = 0.0
-    for e in range(experts):
-        hidden_grad = hidden_grad + dot_nt(g_rows, wout[e]) * mask[e]
     load_in.wait()
-
-    arrived(inputs)
-    inputs = to_group(0)
     arrived(inputs)
     x_rows = rows_of(0)
     pre = 0.0
@@ -240,6 +271,12 @@
         mine = x_rows * mask[e]
         x_o[e] = mine
         pre = pre + dot(mine.astype(BF16), win[e])
+    arrived(grads)
+    g_rows = rows_of(1).astype(BF16)
+    g_o[...] = g_rows
+    hidden_grad = 0.0
+    for e in range(experts):
+        hidden_grad = hidden_grad + dot_nt(g_rows, wout[e]) * mask[e]
     hidden, back = jax.vjp(jax.nn.gelu, pre)
     pre_grad = back(hidden_grad)[0]
 
@@ -264,10 +301,27 @@
     forward = share(0, out_part)
     pg_o[...] = pre_grad.astype(BF16)
 
-    def gather_exp(kind):
+    def send_piece(kind, peers, g, t):
+        copies = []
+        for peer in peers:
+            at = ag.at[kind, par, g, t]
+            copies.append([net.start(at, at, peer)])
+            if kind == 1:
+                at = inn.at[par, g, t]
+                copies[-1].append(net.start(at, at, peer))
+        return copies
+
+    def send_column(kind, t):
+        at = ag.at[kind, par, :, t]
+        copies = [net.start(at, at, pair)]
+        if kind == 1:
+            at = inn.at[par, :, t]
+            copies.append(net.start(at, at, pair))
+        return copies
+
+    def make_piece(kind):
         piece = total_of(buf_e[kind, s], rcv_e.at[kind], seq_n - 1).astype(BF16)
         ag[kind, par, h, s] = piece
-        copies = []
         if kind == 1:
             inner = jnp.sum(piece.astype(F32) * xf[...], axis=2, keepdims=True)
             lane = lax.broadcasted_iota(jnp.int32, inn.shape[3:], 1)
@@ -275,25 +329,8 @@
             for c in range(clips):
                 tile = jnp.where(lane == c, inner[c], tile)
             inn[par, h, s] = tile
-            for peer in exp_peers:
-                copies.append(net.start(inn.at[par, h, s], inn.at[par, h, s], peer))
-        for peer in exp_peers:
-            copies.append(net.start(ag.at[kind, par, h, s], ag.at[kind, par, h, s], peer))
-        return copies
-
-    def gather_seq(kind):
-        copies = []
-        for peer in seq_peers:
-            if kind == 1:
-                copies.append(net.start(inn.at[par, :, s], inn.at[par, :, s], peer))
-            copies.append(net.start(ag.at[kind, par, :, s], ag.at[kind, par, :, s], peer))
-        return copies
-
-    def gather_pair(kind):
-        copies = [net.start(ag.at[kind, par], ag.at[kind, par], pair)]
-        if kind == 1:
-            copies.append(net.start(inn.at[par], inn.at[par], pair))
-        return copies
+        along[kind] = send_piece(kind, exp_peers, h, s)
+        across[kind] = [send_piece(kind, seq_peers, h, s)]
 
     owners = [(q, g) for g in range(half) for q in range(2)]
 
@@ -309,20 +346,27 @@
                 else:
                     wr_o[c, slots:, cut] = value
 
+    along, across, last = {}, {}, {}
     arrived(backward)
-    backward = gather_exp(1)
+    make_piece(1)
     arrived(forward)
-    forward = gather_exp(0)
+    make_piece(0)
     for c in range(clips):
         wr_o[c, :slots] = rt[...]
-    arrived(backward)
-    backward = gather_seq(1)
-    arrived(forward)
-    forward = gather_seq(0)
-    arrived(backward)
-    backward = gather_pair(1)
-    arrived(forward)
-    forward = gather_pair(0)
+    for k in range(half - 1):
+        source = (h + half - 1 - k) % half
+        for kind in (1, 0):
+            arrived(along[kind][k])
+            across[kind].append(send_piece(kind, seq_peers, source, s))
+    for kind in (1, 0):
+        last[kind] = send_column(kind, s)
+    for k in range(seq_n - 1):
+        source = (s + seq_n - 1 - k) % seq_n
+        for kind in (1, 0):
+            for step in across[kind]:
+                arrived(step[k])
+            last[kind] += send_column(kind, source)
+    backward, forward = last[1], last[0]
     arrived(backward)
     write_out(1)
     parts = []
@@ -369,13 +413,16 @@
     gwout[0] = dot(hid[0].T.astype(BF16), g[...]).astype(BF16)
 
 
-def scatter(seq_n, exp_n, gr, out, buf_a, rcv_a, buf_b, rcv_b, buf_c, rcv_c, send_sem, recv_sem):
+def scatter(seq_n, exp_n, gr, out, buf_a, rcv_a, buf_b, rcv_b, send_sem, recv_sem):
     half = exp_n // 2
-    s, h, par, pair, seq_peers, exp_peers = place(seq_n, exp_n)
+    s, h, par, pair, _, _ = place(seq_n, exp_n)
+    ways = [(a, b) for a in range(seq_n) for b in range(half) if a or b]
+    there = [((s + a) % seq_n, (h + b) % half) for a, b in ways]
+    peers = [(t, g * 2 + par) for t, g in there]
     rows, slots = out.shape
-    packed = buf_c.shape[1]
+    packed = buf_b.shape[2]
     pack = rows // packed
-    greet([pair] + seq_peers + exp_peers)
+    greet([pair] + peers)
     net = Sender(send_sem, recv_sem)
     whole = gr[...].T
     for t in range(seq_n):
@@ -384,24 +431,16 @@
                 at = (t * exp_n + 2 * g + q) * rows
                 parts = [whole[at + j * packed : at + (j + 1) * packed] for j in range(pack)]
                 buf_a[q, t, g] = jnp.concatenate(parts, axis=1).astype(BF16)
-    await_greetings([pair] + seq_peers + exp_peers)
+    await_greetings([pair] + peers)
     net.start(buf_a.at[1 - par], rcv_a, pair).wait_recv()
     buf_b[...] = (buf_a[par].astype(F32) + rcv_a[...].astype(F32)).astype(BF16)
-    copies = [net.start(buf_b.at[peer[0]], rcv_b.at[k], peer) for k, peer in enumerate(seq_peers)]
-    for copy in copies:
+    copies = [
+        net.start(buf_b.at[t, g], rcv_b.at[k], peers[k]) for k, (t, g) in enumerate(there)
+    ]
+    total = buf_b[s, h].astype(F32)
+    for k, copy in enumerate(copies):
         copy.wait_recv()
-    total = buf_b[s].astype(F32)
-    for k in range(seq_n - 1):
         total = total + rcv_b[k].astype(F32)
-    buf_c[...] = total.astype(BF16)
-    copies = [
-        net.start(buf_c.at[(h + 1 + k) % half], rcv_c.at[k], peer) for k, peer in enumerate(exp_peers)
-    ]
-    for copy in copies:
-        copy.wait_recv()
-    total = buf_c[h].astype(F32)
-    for k in range(half - 1):
-        total = total + rcv_c[k].astype(F32)
     for j in range(pack):
         out[j * packed : (j + 1) * packed] = total[:, j * slots : (j + 1) * slots]
     net.drain()
@@ -459,7 +498,9 @@
             pltpu.VMEM((2, seq_n - 1) + block, BF16),
             pltpu.VMEM((2, 2, half, seq_n) + block, BF16),
             pltpu.VMEM((2, half, seq_n, owned, 128), F32),
-            pltpu.VMEM((clips, slots, width), F32),
+            pltpu.VMEM((2, half, owned, -(-2 * clips // 8) * 8), F32),
+            pltpu.VMEM((2, half, owned, -(-seq_n * clips // 8) * 8), F32),
+            pltpu.VMEM((2, half, owned, -(-half * clips // 8) * 8), F32),
             pltpu.SemaphoreType.DMA((2 * clips + 2,)),
             pltpu.SemaphoreType.DMA((n_front,)),
             pltpu.SemaphoreType.DMA((n_front,)),
@@ -511,7 +552,7 @@
     )(tokens, grad_out, so, wr, st, x, g, hid, pg)
 
     out_rows = width // (seq_n * exp_n)
-    n_scatter = 1 + (seq_n - 1) + (half - 1)
+    n_scatter = seq_n * half
     pack = max(1, 128 // slots)
     tile = (out_rows // pack, slots * pack)
     grad_router = pl.pallas_call(
@@ -523,9 +564,7 @@
             pltpu.VMEM((2, seq_n, half) + tile, BF16),
             pltpu.VMEM((seq_n, half) + tile, BF16),
             pltpu.VMEM((seq_n, half) + tile, BF16),
-            pltpu.VMEM((seq_n - 1, half) + tile, BF16),
-            pltpu.VMEM((half,) + tile, BF16),
-            pltpu.VMEM((half - 1,) + tile, BF16),
+            pltpu.VMEM((seq_n * half - 1,) + tile, BF16),
             pltpu.SemaphoreType.DMA((n_scatter,)),
             pltpu.SemaphoreType.DMA((n_scatter,)),
         ],

time: 71.9 us -> 67.4 us (0.937)
  Pallas kernels: 69.7 us -> 65.2 us
    pallas_call x1, Pallas kernels: 43.8 us -> 40 us  [on_device(): pl.pallas_call(functools.partial(front, seq_n, exp_n), out_shape=(shape((...]
where the time goes in v3:
time: 67.4 us; the launch traced here: 67.2 us
  Pallas kernels  65.2 us (97%)
  local copies, waits for them, and re-layouts  1.32 us (2%)
    pallas_call x1, Pallas kernels, on_device(): pl.pallas_call(functools.partial(front, seq_n, exp_n), out_shape=(shape((...  40 us
    pallas_call x1, Pallas kernels, on_device(): pl.pallas_call(functools.partial(finish, clips, steps), grid=(steps,), ou...  14.8 us
    pallas_call x1, Pallas kernels, on_device(): pl.pallas_call(functools.partial(scatter, seq_n, exp_n), out_shape=shape(...  10.5 us

profile of v3, /device:TPU:0, one launch (start us, length us, event | category | flops | bytes accessed | tf_op | source)
XLA Modules:
  0.0 67.2 jit_solution(16591899589138203755)
XLA Ops:
  0.6 40.0 %front.1 = (bf16[2,64,1024]{2,1,0:T(8,128)(2,1)}, bf16[2,128,1024]{2,1,0:T(8,128)(2,1)}, f32[8,64]{1,0:T(8,128)}, f32[2,16,1024]{2,1,0:T(8,128)}, bf16[16,1024]{...) custom-call(bf16[2,768,1024]{2,1,0:T(8,128)(2,1)} %tok.1, bf16[64,1024]{1,0:T(8,128)(2,1)} %bitcast.1, ...), custom_call_target="tpu_custom_call" | custom-call | tf_op jit(solution)/shard_map/front/pallas_call | solution.py:463
  40.6 14.8 %finish.1 = (bf16[2,768,1024]{2,1,0:T(8,128)(2,1)}, bf16[2,768,1024]{2,1,0:T(8,128)(2,1)}, f32[64,1024]{1,0:T(8,128)}, bf16[2,1024,1024]{2,1,0:T(8,128)(2,1)}, bf16[2,1024,1024]{2,1,0:T(8,128)(2,1)}) custom-call(bf16[2,768,1024]{2,1,0:T(8,128)(2,1)} %tok.1, bf16[2,768,1024]{2,1,0:T(8,128)(2,1)} %gout.1, bf16[2,64,1024]{2,1,0:T(8,128)(2,1)} %get-tuple-element.17.so, ...), custom_call_target="tpu_custom_call" | custom-call | tf_op jit(solution)/shard_map/finish/pallas_call | solution.py:523
  55.4 10.5 %scatter.1 = f32[32,64]{1,0:T(8,128)} custom-call(f32[64,1024]{1,0:T(8,128)} %get-tuple-element.26.gr), custom_call_target="tpu_custom_call" | custom-call | tf_op jit(solution)/shard_map/scatter/pallas_call | solution.py:558
  65.9 1.3 %copy.11 = f32[32,64]{1,0:T(8,128)} copy(f32[32,64]{1,0:T(8,128)} %scatter.1) | data formatting | bytes 16384

commit v4 on v3

--- a/solution.py
+++ b/solution.py
@@ -112,9 +112,6 @@
     peaks, masses = [], []
     for c in range(clips):
         load_tok[c].wait()
-        if c == clips - 1:
-            load_out.start()
-            load_in.start()
         lg = dot_nt(tok[c], rt[...])
         m = jnp.max(lg, axis=0, keepdims=True)
         p = jnp.exp(lg - m)
@@ -242,6 +239,8 @@
     for c in range(1, clips):
         load_gout[c].wait()
         lay_out(dot(qt[c], gout[c]), 1, c)
+    load_in.start()
+    load_out.start()
     grads = to_pair(1)
     arrived(stat)
     st_c[...] = combine([st_b[...]] + [st_s[k] for k in range(seq_n - 1)])
@@ -262,8 +261,8 @@
     row = lax.broadcasted_iota(jnp.int32, (n_rows, 1), 0)
     expert_of = (row % owned) // (owned // experts)
     mask = [(expert_of == e).astype(F32) for e in range(experts)]
+    load_in.wait()
     load_out.wait()
-    load_in.wait()
     arrived(inputs)
     x_rows = rows_of(0)
     pre = 0.0
@@ -271,14 +270,7 @@
         mine = x_rows * mask[e]
         x_o[e] = mine
         pre = pre + dot(mine.astype(BF16), win[e])
-    arrived(grads)
-    g_rows = rows_of(1).astype(BF16)
-    g_o[...] = g_rows
-    hidden_grad = 0.0
-    for e in range(experts):
-        hidden_grad = hidden_grad + dot_nt(g_rows, wout[e]) * mask[e]
     hidden, back = jax.vjp(jax.nn.gelu, pre)
-    pre_grad = back(hidden_grad)[0]
 
     def share(kind, part):
         for t in range(seq_n):
@@ -289,17 +281,12 @@
             for k, peer in enumerate(seq_peers)
         ]
 
-    in_part = 0.0
-    for e in range(experts):
-        in_part = in_part + dot_nt((pre_grad * mask[e]).astype(BF16), win[e])
-    backward = share(1, in_part)
     out_part = 0.0
     for e in range(experts):
         mine = hidden * mask[e]
         hid_o[e] = mine
         out_part = out_part + dot(mine.astype(BF16), wout[e])
     forward = share(0, out_part)
-    pg_o[...] = pre_grad.astype(BF16)
 
     def send_piece(kind, peers, g, t):
         copies = []
@@ -347,26 +334,41 @@
                     wr_o[c, slots:, cut] = value
 
     along, across, last = {}, {}, {}
-    arrived(backward)
-    make_piece(1)
+    arrived(grads)
+    g_rows = rows_of(1).astype(BF16)
+    g_o[...] = g_rows
+    hidden_grad = 0.0
+    for e in range(experts):
+        hidden_grad = hidden_grad + dot_nt(g_rows, wout[e]) * mask[e]
     arrived(forward)
     make_piece(0)
+    pre_grad = back(hidden_grad)[0]
+    in_part = 0.0
+    for e in range(experts):
+        in_part = in_part + dot_nt((pre_grad * mask[e]).astype(BF16), win[e])
+    backward = share(1, in_part)
+    pg_o[...] = pre_grad.astype(BF16)
     for c in range(clips):
         wr_o[c, :slots] = rt[...]
     for k in range(half - 1):
-        source = (h + half - 1 - k) % half
-        for kind in (1, 0):
-            arrived(along[kind][k])
-            across[kind].append(send_piece(kind, seq_peers, source, s))
-    for kind in (1, 0):
+        arrived(along[0][k])
+        across[0].append(send_piece(0, seq_peers, (h + half - 1 - k) % half, s))
+    arrived(backward)
+    make_piece(1)
+    for k in range(half - 1):
+        arrived(along[1][k])
+        across[1].append(send_piece(1, seq_peers, (h + half - 1 - k) % half, s))
+    for kind in (0, 1):
         last[kind] = send_column(kind, s)
     for k in range(seq_n - 1):
         source = (s + seq_n - 1 - k) % seq_n
-        for kind in (1, 0):
+        for kind in (0, 1):
             for step in across[kind]:
                 arrived(step[k])
             last[kind] += send_column(kind, source)
     backward, forward = last[1], last[0]
+    arrived(forward)
+    write_out(0)
     arrived(backward)
     write_out(1)
     parts = []
@@ -380,8 +382,6 @@
     st_o[...] = jnp.concatenate(
         [stats[: 2 * clips]] + inners + [jnp.zeros((8 - 3 * clips, slots), F32)], axis=0
     )
-    arrived(forward)
-    write_out(0)
     net.drain()
 
 
@@ -509,7 +509,7 @@
         name="front",
     )(tokens, router_t, grad_out, w_in, w_out)
 
-    steps = 4 * clips
+    steps = 2 * clips
     t_blocks = steps // clips
     w_blocks = steps // experts
     token_spec = pl.BlockSpec((1, rows // t_blocks, width), lambda i: (i // t_blocks, i % t_blocks, 0))

time: 67.4 us -> 65.8 us (0.976)
  Pallas kernels: 65.2 us -> 63.6 us
    pallas_call x1, Pallas kernels: 14.8 us -> 12.2 us  [on_device(): pl.pallas_call(functools.partial(finish, clips, steps), grid=(steps,), ou...]
    pallas_call x1, Pallas kernels: 40 us -> 40.8 us  [on_device(): pl.pallas_call(functools.partial(front, seq_n, exp_n), out_shape=(shape((...]
where the time goes in v4:
time: 65.8 us; the launch traced here: 65.6 us
  Pallas kernels  63.6 us (97%)
  local copies, waits for them, and re-layouts  1.32 us (2%)
    pallas_call x1, Pallas kernels, on_device(): pl.pallas_call(functools.partial(front, seq_n, exp_n), out_shape=(shape((...  40.8 us
    pallas_call x1, Pallas kernels, on_device(): pl.pallas_call(functools.partial(finish, clips, steps), grid=(steps,), ou...  12.2 us
    pallas_call x1, Pallas kernels, on_device(): pl.pallas_call(functools.partial(scatter, seq_n, exp_n), out_shape=shape(...  10.5 us
    unnamed x1, local copies, waits for them, and re-layouts  1.32 us

profile of v4, /device:TPU:0, one launch (start us, length us, event | category | flops | bytes accessed | tf_op | source)
XLA Modules:
  0.0 65.6 jit_solution(12035692796979803852)
XLA Ops:
  0.6 40.8 %front.1 = (bf16[2,64,1024]{2,1,0:T(8,128)(2,1)}, bf16[2,128,1024]{2,1,0:T(8,128)(2,1)}, f32[8,64]{1,0:T(8,128)}, f32[2,16,1024]{2,1,0:T(8,128)}, bf16[16,1024]{...) custom-call(bf16[2,768,1024]{2,1,0:T(8,128)(2,1)} %tok.1, bf16[64,1024]{1,0:T(8,128)(2,1)} %bitcast.1, ...), custom_call_target="tpu_custom_call" | custom-call | tf_op jit(solution)/shard_map/front/pallas_call | solution.py:463
  41.5 12.2 %finish.1 = (bf16[2,768,1024]{2,1,0:T(8,128)(2,1)}, bf16[2,768,1024]{2,1,0:T(8,128)(2,1)}, f32[64,1024]{1,0:T(8,128)}, bf16[2,1024,1024]{2,1,0:T(8,128)(2,1)}, bf16[2,1024,1024]{2,1,0:T(8,128)(2,1)}) custom-call(bf16[2,768,1024]{2,1,0:T(8,128)(2,1)} %tok.1, bf16[2,768,1024]{2,1,0:T(8,128)(2,1)} %gout.1, bf16[2,64,1024]{2,1,0:T(8,128)(2,1)} %get-tuple-element.17.so, ...), custom_call_target="tpu_custom_call" | custom-call | tf_op jit(solution)/shard_map/finish/pallas_call | solution.py:523
  53.7 10.5 %scatter.1 = f32[32,64]{1,0:T(8,128)} custom-call(f32[64,1024]{1,0:T(8,128)} %get-tuple-element.26.gr), custom_call_target="tpu_custom_call" | custom-call | tf_op jit(solution)/shard_map/scatter/pallas_call | solution.py:558
  64.2 1.3 %copy.11 = f32[32,64]{1,0:T(8,128)} copy(f32[32,64]{1,0:T(8,128)} %scatter.1) | data formatting | bytes 16384
